TPU v7x, 256 devices: a whole 4x4x8 slice. The times are simulated.
256 devices in a mesh: pop: 64 (over x, z, core), mp: 4 (over y).
Axes of the slice: x: 4, y: 4, z: 8, core: 2. Of those that a mesh axis runs over, the one named last changes fastest.
Arguments:
- tokens: bfloat16 [256, 3584], replicated, may hold values from -60 to 60
- target: bfloat16 [256, 3584], P(None, 'mp'), may hold values from -6 to 6
- w_query: bfloat16 [3584, 3584], P('pop', 'mp'), may hold values from -0.09375 to 0.09375
- w_key: bfloat16 [3584, 512], P(None, 'mp'), may hold values from -0.09375 to 0.09375
- w_value: bfloat16 [3584, 512], P(None, 'mp'), may hold values from -0.09375 to 0.09375
- w_out: bfloat16 [3584, 3584], P('mp', 'pop'), may hold values from -0.09375 to 0.09375
- query_left_factors: bfloat16 [64, 3584, 4], P('pop'), may hold values from -0.09375 to 0.09375
- query_right_factors: bfloat16 [64, 4, 3584], P('pop', None, 'mp'), may hold values from -6 to 6
- o_left: bfloat16 [64, 3584, 4], P('pop', 'mp'), may hold values from -0.09375 to 0.09375
- o_right: bfloat16 [64, 4, 3584], P('pop'), may hold values from -6 to 6
- member_ids: int32 [64], P('pop'), may hold values from 0 to 63, each once
Outputs:
- grad_query: float32 [3584, 3584], P('pop', 'mp')
- grad_out: float32 [3584, 3584], P('mp', 'pop')
- fitness: float32 [64], P('pop')
Inputs may be any that keep to these rules, and one draw needn't show every extreme that they name: `member_ids`: every number from 0 to 63 appears once.
All inputs are finite; a program needn't handle non-finite values.
Results may differ from a plain program's by a relative error of at most 0.005.
Values may be sent and summed in bfloat16 or wider, within the bound.
No kernel may reach another device: no remote copies, remote signals or barrier semaphores. Data moves between devices by JAX's collectives and lax.ppermute only.
A program may use at most 64 MiB of HBM per device.

v0:
```python
import math
import jax
import jax.numpy as jnp
from jax import lax
from jax.sharding import Mesh
from jax.sharding import PartitionSpec as P

D = 3584
HEADS = 28
KV_HEADS = 4
HEAD_DIM = 128
RANK = 4
POP = ("pop_0", "pop_1", "pop_2")
noise_scale = 0.5
rope_base = 1000000.0
spread_floor = 0.001


def in_order(parts, dim):
    parts = jnp.moveaxis(parts, 0, dim)
    shape = parts.shape
    return parts.reshape(*shape[:dim], shape[dim] * shape[dim + 1], *shape[dim + 2 :])


def all_blocks(shard, axes, turns):
    parts = shard[None]
    for k in turns:
        parts = lax.all_gather(parts, axes[k], axis=0, tiled=True)
    held = [lax.axis_size(axes[k]) for k in reversed(turns)]
    parts = parts.reshape(*held, *shard.shape)
    turned = sorted(range(len(turns)), key=lambda place: turns[len(turns) - 1 - place])
    return parts.transpose(*turned, *range(len(turns), parts.ndim)).reshape(-1, *shard.shape)


def whole_of(shard, axes, turns, dim):
    return in_order(all_blocks(shard, axes, turns), dim)


def cut_along(shard, dim, devices):
    before, after = (shard.shape[:dim], shard.shape[dim + 1 :])
    return jnp.moveaxis(shard.reshape(*before, devices, -1, *after), dim, 0)


def summed_on_arrival(shard, axis, dim):
    devices = lax.axis_size(axis)
    parts = lax.all_to_all(cut_along(shard, dim, devices), axis, 0, 0, tiled=True)
    return jnp.sum(parts.astype(jnp.float32), axis=0)


def copy_for_each(shard, axis):
    copies = jnp.broadcast_to(shard, (lax.axis_size(axis), *shard.shape))
    return lax.all_to_all(copies, axis, split_axis=0, concat_axis=0, tiled=True)


def of_everyone(shard, axis):
    return copy_for_each(shard, axis).sum(axis=0)


def gathered_copies(shard, axis, dim):
    return in_order(copy_for_each(shard, axis), dim)


def side_by_side(arrays, axis, dim, along):
    columns = [a.reshape(*a.shape[:along], -1) for a in arrays]
    both = jnp.concatenate(columns, axis=along)
    result, at, done = (lax.all_gather(both, axis, axis=dim, tiled=True), 0, [])
    for a, column in zip(arrays, columns):
        share = result[..., at : at + column.shape[along]]
        done.append(share.reshape(*share.shape[:along], *a.shape[along:]))
        at += column.shape[along]
    return tuple(done)


def tables(count, head_size):
    position = jnp.arange(count, dtype=jnp.float32)
    index = jnp.arange(head_size // 2, dtype=jnp.float32)
    freq = jnp.exp(-math.log(rope_base) * 2.0 * index / head_size)
    angle = position[:, None] * freq[None, :]
    return (jnp.cos(angle)[:, None, :], jnp.sin(angle)[:, None, :])


def rotate(field, cosine_table, sine):
    half = field.shape[-1] // 2
    first = field[..., :half]
    second = field[..., half:]
    return jnp.concatenate(
        [first * cosine_table - second * sine, second * cosine_table + first * sine], axis=-1
    )


def per_device(
    tokens,
    target,
    w_query,
    w_key,
    w_value,
    w_out,
    query_left_factors,
    query_right_factors,
    o_left,
    o_right,
    member_ids,
):
    tok = tokens.shape[0]
    local_feats = w_query.shape[1]
    local_kv = w_key.shape[1] // HEAD_DIM
    group = HEADS // KV_HEADS
    local_heads = local_kv * group
    slots = query_left_factors.shape[0]
    scale = HEAD_DIM ** (-0.5)
    cosine_table, sine = tables(tok, HEAD_DIM)
    base = jnp.dot(tokens, whole_of(w_query, POP, (0, 1, 2), 0), preferred_element_type=jnp.float32)
    keys = rotate(
        jnp.dot(tokens, w_key, preferred_element_type=jnp.float32).reshape(tok, local_kv, HEAD_DIM),
        cosine_table,
        sine,
    ).astype(jnp.bfloat16)
    values = (
        jnp.dot(tokens, w_value, preferred_element_type=jnp.float32)
        .astype(jnp.bfloat16)
        .reshape(tok, local_kv, HEAD_DIM)
    )
    signs = (1 - 2 * (member_ids % 2)).astype(jnp.float32)
    factor = noise_scale * signs[:, None, None]
    lowrank_product = jnp.einsum(
        "td,mdr->mtr", tokens, query_left_factors, preferred_element_type=jnp.float32
    ).astype(jnp.bfloat16)
    query = base[None] + factor * jnp.einsum(
        "olj,ojv->olv", lowrank_product, query_right_factors, preferred_element_type=jnp.float32
    )
    query = rotate(
        query.reshape(slots, tok, local_heads, HEAD_DIM), cosine_table[None], sine[None]
    ).astype(jnp.bfloat16)
    query = query.reshape(slots, tok, local_kv, group, HEAD_DIM)
    scores = jnp.einsum("mtkgd,skd->mkgts", query, keys, preferred_element_type=jnp.float32) * scale
    causal = jnp.arange(tok)[:, None] >= jnp.arange(tok)[None, :]
    scores = jnp.where(causal, scores, -1e30)
    probs = jax.nn.softmax(scores, axis=-1).astype(jnp.bfloat16)
    mixed = (
        jnp.einsum("mkgts,skd->mtkgd", probs, values, preferred_element_type=jnp.float32)
        .astype(jnp.bfloat16)
        .reshape(slots, tok, local_feats)
    )
    low_out = jnp.einsum("mtf,mfr->mtr", mixed, o_left, preferred_element_type=jnp.float32)
    right_full = o_right.astype(jnp.float32)
    part = jnp.einsum(
        "mtf,fe->mte",
        mixed,
        lax.all_gather(w_out, POP, axis=1, tiled=True),
        preferred_element_type=jnp.float32,
    )
    term = part + factor * jnp.einsum(
        "mtr,mre->mte", low_out, right_full, precision=lax.Precision.HIGHEST
    )
    output = summed_on_arrival(term.astype(jnp.bfloat16), "mp", 2)
    diff = output - target.astype(jnp.float32)[None]
    errors = of_everyone(jnp.sum(diff * diff, axis=(1, 2)), "mp")
    fitness = -(errors / (tok * D))
    count = slots * lax.axis_size(POP)
    everyone = gathered_copies(fitness, POP, 0)
    mean = jnp.sum(everyone) / count
    spread = jnp.sum((everyone - mean) * (everyone - mean)) / count
    weight = signs * (fitness - mean) / jnp.sqrt(spread + spread_floor)
    every_weight = gathered_copies(weight, POP, 0)
    right_factors_gathered, left_all = side_by_side((query_right_factors, o_left), POP, 0, 1)
    rows_q = lax.all_to_all(query_left_factors, POP, split_axis=1, concat_axis=0, tiled=True)
    cols_o = lax.all_to_all(o_right, POP, split_axis=2, concat_axis=0, tiled=True)
    whole_population = rows_q.shape[0]
    left_q = jnp.transpose(
        rows_q.astype(jnp.float32) * every_weight[:, None, None], (1, 0, 2)
    ).reshape(rows_q.shape[1], whole_population * RANK)
    right_q = right_factors_gathered.astype(jnp.float32).reshape(
        whole_population * RANK, local_feats
    )
    grad_query = jnp.dot(left_q, right_q, precision=lax.Precision.HIGHEST) / noise_scale
    output_left_factor = jnp.transpose(
        left_all.astype(jnp.float32) * every_weight[:, None, None], (1, 0, 2)
    ).reshape(local_feats, whole_population * RANK)
    right_o = cols_o.astype(jnp.float32).reshape(whole_population * RANK, cols_o.shape[2])
    grad_out = jnp.dot(output_left_factor, right_o, precision=lax.Precision.HIGHEST) / noise_scale
    return (grad_query, grad_out, fitness)


def solution(mesh):
    torus = Mesh(mesh.devices.reshape(4, 8, 2, mesh.shape["mp"]), ("pop_0", "pop_1", "pop_2", "mp"))
    placed = (
        P(),
        P(None, "mp"),
        P(POP, "mp"),
        P(None, "mp"),
        P(None, "mp"),
        P("mp", POP),
        P(POP, None, None),
        P(POP, None, "mp"),
        P(POP, "mp", None),
        P(POP, None, None),
        P(POP),
    )
    return jax.shard_map(
        per_device,
        mesh=torus,
        in_specs=placed,
        out_specs=(P(POP, "mp"), P("mp", POP), P(POP)),
        check_vma=False,
    )
```

profile of v0, /device:TPU:1, one launch (start us, length us, event | category | flops | bytes accessed | tf_op | source)
XLA Modules:
  0.0 428.7 jit_solution(7784847421207332163)
XLA Ops:
  7.2 13.0 %all-gather = bf16[224,896]{1,0:T(8,128)(2,1)} all-gather(bf16[56,896]{1,0:T(8,128)(2,1)} %param.13), channel_id=2, replica_groups=mesh['pop_0'=4,'pop_1'=8,'pop_2'=2,'mp'=4] {'pop_0'}, dimensions={0}, use_global_device_ids=true | all-gather | bytes 501760 | tf_op jit(solution)/shard_map/all_gather | solution.py:28
  20.3 49.6 %all-gather.6.cloned.1.call-done = bf16[32,56,896]{2,1,0:T(8,128)(2,1)} async-done(((bf16[4,56,896]{2,1,0:T(8,128)(2,1)}), bf16[32,56,896]{2,1,0:T(8,128)(2,1)}) %all-gather.6.cloned.1.call-update) | async-done | bytes 3211280 | tf_op jit(solution)/shard_map/all_gather | solution.py:28
  73.6 19.9 %all-gather.8.cloned.1.call-done = bf16[64,56,896]{2,1,0:T(8,128)(2,1)} async-done(((bf16[32,56,896]{2,1,0:T(8,128)(2,1)}), bf16[64,56,896]{2,1,0:T(8,128)(2,1)}) %all-gather.8.cloned.1.call-update) | async-done | bytes 6422544 | tf_op jit(solution)/shard_map/all_gather | solution.py:28
  93.5 3.3 copy.114
  96.9 2.1 fusion.29
  99.1 2.1 fusion.3
  101.1 1.5 copy.115
  110.0 2.6 convolution_convert_fusion
  112.8 65.1 %all-gather.10.cloned.1.call-done = bf16[896,3584]{0,1:T(8,128)(2,1)} async-done(((bf16[896,56]{0,1:T(8,128)(2,1)}), bf16[896,3584]{0,1:T(8,128)(2,1)}) %all-gather.10.cloned.1.call-update) | async-done | bytes 6422544 | tf_op jit(solution)/shard_map/all_gather | solution.py:149
  177.9 4.9 %fusion.30 = f32[256,3584]{1,0:T(8,128)S(1)} fusion(bf16[256,896]{0,1:T(8,128)(2,1)S(1)} %bitcast.106, bf16[896,3584]{0,1:T(8,128)(2,1)} %all-gather.10.cloned.1.call-done), kind=kOutput, calls=%fused_computation.58 | convolution fusion | flops 1644167168 | bytes 10551296 | tf_op jit(solution)/shard_map/mtf,fe->mte/dot_general | solution.py:146
  182.8 3.1 fusion.1
  185.9 3.3 reshape.288
  189.2 1.5 copy.145
  190.7 4.0 all-to-all-start.1
  195.3 22.5 %all-to-all-done.1 = bf16[4,1,256,896]{3,2,1,0:T(8,128)(2,1)S(1)} async-done(((bf16[4,1,256,896]{3,2,1,0:T(8,128)(2,1)}), bf16[4,1,256,896]{3,2,1,0:T(8,128)(2,1)S(1)}, u32[]{:S(2)}, u32[]{:S(2)}) %all-to-all-start.1) | async-done | bytes 1835040 | tf_op jit(solution)/shard_map/all_to_all | solution.py:46
  219.6 6.5 %all_to_all.47 = f32[4,1,1]{2,1,0:T(1,128)S(1)} all-to-all(f32[4,1,1]{2,1,0:T(1,128)S(1)} %broadcast_in_dim.34), channel_id=1, replica_groups=mesh['pop_0'=4,'pop_1'=8,'pop_2'=2,'mp'=4] {'mp'}, dimensions={0} | all-to-all | bytes 32 | tf_op jit(solution)/shard_map/all_to_all | solution.py:52
  227.9 7.9 %all-to-all-start.3 = ((f32[64,1,1]{2,1,0:T(1,128)}), f32[64,1,1]{2,1,0:T(1,128)S(1)}, u32[]{:S(2)}, u32[]{:S(2)}) async-start(f32[64,1,1]{2,1,0:T(1,128)} %broadcast_in_dim.35), calls=%async_computation.3 | async-start | bytes 65536 | tf_op jit(solution)/shard_map/all_to_all | solution.py:52
  235.9 51.8 %all-gather.1 = bf16[64,1,7168]{2,1,0:T(2,128)(2,1)S(1)} all-gather(bf16[1,1,7168]{2,1,0:T(2,128)(2,1)S(1)} %maximum_bitcast_fusion.2), channel_id=1, replica_groups=mesh['pop_0'=4,'pop_1'=8,'pop_2'=2,'mp'=4] {'pop_0','pop_1','pop_2'}, dimensions={0}, use_global_device_ids=true | all-gather | bytes 931840 | tf_op jit(solution)/shard_map/all_gather | solution.py:66
  287.7 3.2 copy.129
  292.2 7.3 %all-to-all-start.5 = ((bf16[1,4,3584]{1,0,2:T(2,128)(2,1)}), bf16[1,4,3584]{1,0,2:T(2,128)(2,1)S(1)}, u32[]{:S(2)}, u32[]{:S(2)}) async-start(bf16[1,4,3584]{1,0,2:T(2,128)(2,1)} %copy.129), calls=%async_computation.5 | async-start | bytes 3670016 | tf_op jit(solution)/shard_map/all_to_all | solution.py:167
  299.4 2.0 slice_convert_fusion
  301.5 3.2 copy.112
  306.1 38.7 %all-to-all-done.5 = bf16[1,4,3584]{1,0,2:T(2,128)(2,1)S(1)} async-done(((bf16[1,4,3584]{1,0,2:T(2,128)(2,1)}), bf16[1,4,3584]{1,0,2:T(2,128)(2,1)S(1)}, u32[]{:S(2)}, u32[]{:S(2)}) %all-to-all-start.5) | async-done | bytes 28704 | tf_op jit(solution)/shard_map/all_to_all | solution.py:167
  344.8 6.2 %all-to-all-start = ((bf16[1,3584,4]{2,0,1:T(2,128)(2,1)}), bf16[1,3584,4]{2,0,1:T(2,128)(2,1)}, u32[]{:S(2)}, u32[]{:S(2)}) async-start(bf16[1,3584,4]{2,0,1:T(2,128)(2,1)} %copy.112), calls=%async_computation | async-start | bytes 3670016 | tf_op jit(solution)/shard_map/all_to_all | solution.py:166
  352.3 44.0 %all-to-all-done = bf16[1,3584,4]{2,0,1:T(2,128)(2,1)} async-done(((bf16[1,3584,4]{2,0,1:T(2,128)(2,1)}), bf16[1,3584,4]{2,0,1:T(2,128)(2,1)}, u32[]{:S(2)}, u32[]{:S(2)}) %all-to-all-start) | async-done | bytes 28704 | tf_op jit(solution)/shard_map/all_to_all | solution.py:166
  396.9 6.0 %all-to-all-start.4 = ((f32[64,1,1]{2,1,0:T(1,128)}), f32[64,1,1]{2,1,0:T(1,128)S(1)}, u32[]{:S(2)}, u32[]{:S(2)}) async-start(f32[64,1,1]{2,1,0:T(1,128)} %broadcast_in_dim.36), calls=%async_computation.4 | async-start | bytes 65536 | tf_op jit(solution)/shard_map/all_to_all | solution.py:52
  403.0 1.8 copy.127
  406.0 1.8 copy.130
  408.1 3.7 copy.113
  412.8 1.6 multiply_bitcast_fusion
  414.4 2.8 copy.128
  417.2 1.5 reshape.293
  (71 shorter events, 22.1 us)
Async XLA Ops:
  7.2 64.2 %copy-start = (bf16[256,3584]{1,0:T(8,128)(2,1)S(1)}, bf16[256,3584]{1,0:T(8,128)(2,1)}, u32[]{:S(2)}) copy-start(bf16[256,3584]{1,0:T(8,128)(2,1)} %param.11) | copy-start | bytes 5505028
  7.2 62.7 %all-gather.6.cloned.1.call-start = ((), (), s32[]{:S(2)}) async-start(), calls=%async_computation.6 | async-start | bytes 3612672 | tf_op jit(solution)/shard_map/all_gather | solution.py:28
  20.2 51.2 %copy-start.4 = (bf16[3584,128]{1,0:T(8,128)(2,1)S(1)}, bf16[3584,128]{1,0:T(8,128)(2,1)}, u32[]{:S(2)}) copy-start(bf16[3584,128]{1,0:T(8,128)(2,1)} %param.14) | copy-start | bytes 2752516
  20.3 73.3 %all-gather.8.cloned.1.call-start = ((), (), s32[]{:S(2)}) async-start(), calls=%async_computation.7 | async-start | bytes 9633792 | tf_op jit(solution)/shard_map/all_gather | solution.py:28
  69.9 107.9 %all-gather.10.cloned.1.call-start = ((), (), s32[]{:S(2)}) async-start(), calls=%async_computation.8 | async-start | bytes 6522880 | tf_op jit(solution)/shard_map/all_gather | solution.py:149
  96.9 2.2 copy-start.9
  96.9 2.2 copy-start.11
  106.1 1.4 copy-start.6
  106.1 1.4 copy-start.7
  108.1 1.3 copy-start.2
  108.2 1.9 copy-start.13
  110.0 2.6 copy-start.12
  112.8 70.0 %copy-start.8 = (bf16[1,4,3584]{2,1,0:T(4,128)(2,1)S(1)}, bf16[1,4,3584]{2,1,0:T(4,128)(2,1)}, u32[]{:S(2)}) copy-start(bf16[1,4,3584]{2,1,0:T(4,128)(2,1)} %param.20) | copy-start | bytes 86020
  190.7 27.1 %all-to-all-start.1 = ((bf16[4,1,256,896]{3,2,1,0:T(8,128)(2,1)}), bf16[4,1,256,896]{3,2,1,0:T(8,128)(2,1)S(1)}, u32[]{:S(2)}, u32[]{:S(2)}) async-start(bf16[4,1,256,896]{3,2,1,0:T(8,128)(2,1)} %bitcast.98), calls=%async_computation.1 | async-start | bytes 3670016 | tf_op jit(solution)/shard_map/all_to_all | solution.py:46
  194.7 23.3 %copy-start.5 = (bf16[256,896]{1,0:T(8,128)(2,1)S(1)}, bf16[256,896]{1,0:T(8,128)(2,1)}, u32[]{:S(2)}) copy-start(bf16[256,896]{1,0:T(8,128)(2,1)} %param.12) | copy-start | bytes 1376260
  227.9 64.2 %all-to-all-start.3 = ((f32[64,1,1]{2,1,0:T(1,128)}), f32[64,1,1]{2,1,0:T(1,128)S(1)}, u32[]{:S(2)}, u32[]{:S(2)}) async-start(f32[64,1,1]{2,1,0:T(1,128)} %broadcast_in_dim.35), calls=%async_computation.3 | async-start | bytes 65536 | tf_op jit(solution)/shard_map/all_to_all | solution.py:52
  292.2 52.6 %all-to-all-start.5 = ((bf16[1,4,3584]{1,0,2:T(2,128)(2,1)}), bf16[1,4,3584]{1,0,2:T(2,128)(2,1)S(1)}, u32[]{:S(2)}, u32[]{:S(2)}) async-start(bf16[1,4,3584]{1,0,2:T(2,128)(2,1)} %copy.129), calls=%async_computation.5 | async-start | bytes 3670016 | tf_op jit(solution)/shard_map/all_to_all | solution.py:167
  299.4 2.1 copy-start.10
  344.8 51.5 %all-to-all-start = ((bf16[1,3584,4]{2,0,1:T(2,128)(2,1)}), bf16[1,3584,4]{2,0,1:T(2,128)(2,1)}, u32[]{:S(2)}, u32[]{:S(2)}) async-start(bf16[1,3584,4]{2,0,1:T(2,128)(2,1)} %copy.112), calls=%async_computation | async-start | bytes 3670016 | tf_op jit(solution)/shard_map/all_to_all | solution.py:166
  396.9 15.3 %all-to-all-start.4 = ((f32[64,1,1]{2,1,0:T(1,128)}), f32[64,1,1]{2,1,0:T(1,128)S(1)}, u32[]{:S(2)}, u32[]{:S(2)}) async-start(f32[64,1,1]{2,1,0:T(1,128)} %broadcast_in_dim.36), calls=%async_computation.4 | async-start | bytes 65536 | tf_op jit(solution)/shard_map/all_to_all | solution.py:52
  407.9 4.9 %copy-start.3 = (f32[64,3584]{0,1:T(8,128)S(1)}, f32[64,3584]{0,1:T(8,128)}, u32[]{:S(2)}) copy-start(f32[64,3584]{0,1:T(8,128)} %copy.127) | copy-start | bytes 2752516
  414.3 6.7 %copy-start.1 = (bf16[256,3584]{1,0:T(8,128)(2,1)S(1)}, bf16[256,3584]{1,0:T(8,128)(2,1)}, u32[]{:S(2)}) copy-start(bf16[256,3584]{1,0:T(8,128)(2,1)} %param.11) | copy-start | bytes 5505028
Sparse Core Ops, SparseCore 0:
  20.4 49.4 all-gather.5
  71.7 21.7 all-gather.7
  96.2 81.5 all-gather.9
where the time goes:
time: 430 us; the launch traced here: 429 us
  waiting for transfers between devices  241 us (56%)
  blocking collectives  71.3 us (17%)
  local copies, waits for them, and re-layouts  38.2 us (9%)
  starting transfers between devices  31.5 us (7%)
  matrix products  18.6 us (4%)
  between operations  17.9 us (4%)
  other arithmetic  10.5 us (2%)
    all_gather x2, waiting for transfers between devices, all_blocks(): parts = lax.all_gather(parts, axes[k], axis=0, tiled=True)  69.5 us
    all_gather x1, waiting for transfers between devices, per_device(): lax.all_gather(w_out, POP, axis=1, tiled=True)  65.1 us
    all_gather x1, blocking collectives, side_by_side(): result, at, done = (lax.all_gather(both, axis, axis=dim, tiled=True), 0, [])  51.8 us
    all_to_all x1, waiting for transfers between devices, per_device(): lax.all_to_all(query_left_factors, POP, split_axis=1, concat_axis=0, tile...  44 us
    all_to_all x1, waiting for transfers between devices, per_device(): lax.all_to_all(o_right, POP, split_axis=2, concat_axis=0, tiled=True)  38.7 us
    all_to_all x1, waiting for transfers between devices, summed_on_arrival(): lax.all_to_all(cut_along(shard, dim, devices), axis, 0, 0, tiled=True)  22.5 us
    all_to_all x2, starting transfers between devices, copy_for_each(): return lax.all_to_all(copies, axis, split_axis=0, concat_axis=0, tiled=True)  14 us
    all_gather x1, blocking collectives, all_blocks(): parts = lax.all_gather(parts, axes[k], axis=0, tiled=True)  13 us
  transfers between devices with their start and end apart: 8, of which 7 were waited for; matrix products, arithmetic and copies ran while one was open for 9% of the time, Pallas kernels for 0%

commit v1 on v0

--- a/solution.py
+++ b/solution.py
@@ -16,6 +16,13 @@
 spread_floor = 0.001
 
 
+def build_array(message, axis_tag, at_axis):
+    row_out = lax.axis_size(axis_tag)
+    val = jnp.stack(row_out * [message], 0)
+    parts_out = lax.all_to_all(val, axis_tag, split_axis=0, concat_axis=0)
+    return jnp.concatenate(parts_out, at_axis)
+
+
 def in_order(parts, dim):
     parts = jnp.moveaxis(parts, 0, dim)
     shape = parts.shape
@@ -25,7 +32,7 @@
 def all_blocks(shard, axes, turns):
     parts = shard[None]
     for k in turns:
-        parts = lax.all_gather(parts, axes[k], axis=0, tiled=True)
+        parts = build_array(parts, axes[k], 0)
     held = [lax.axis_size(axes[k]) for k in reversed(turns)]
     parts = parts.reshape(*held, *shard.shape)
     turned = sorted(range(len(turns)), key=lambda place: turns[len(turns) - 1 - place])

time: 430 us -> 404 us (0.940)
  waiting for transfers between devices: 241 us -> 194 us
  blocking collectives: 71.3 us -> 81.4 us
  starting transfers between devices: 31.5 us -> 39.2 us
    all_to_all x0 -> x1, waiting for transfers between devices: none -> 87.4 us  [build_array(): parts_out = lax.all_to_all(val, axis_tag, split_axis=0, concat_axis=0)]
    all_gather x2 -> x0, waiting for transfers between devices: 69.5 us -> none  [all_blocks(): parts = lax.all_gather(parts, axes[k], axis=0, tiled=True)]
    all_gather x1, waiting for transfers between devices: 65.1 us -> 0.01 us  [per_device(): lax.all_gather(w_out, POP, axis=1, tiled=True)]
    all_to_all x0 -> x2, blocking collectives: none -> 22.9 us  [build_array(): parts_out = lax.all_to_all(val, axis_tag, split_axis=0, concat_axis=0)]
    all_gather x1 -> x0, blocking collectives: 13 us -> none  [all_blocks(): parts = lax.all_gather(parts, axes[k], axis=0, tiled=True)]
    all_to_all x0 -> x1, starting transfers between devices: none -> 8.31 us  [build_array(): parts_out = lax.all_to_all(val, axis_tag, split_axis=0, concat_axis=0)]
  transfers between devices with their start and end apart: 8 -> 7, of which waited for: 7 -> 5; matrix products, arithmetic and copies ran while one was open for 9% -> 11% of each run, Pallas kernels for 0% -> 0%
where the time goes in v1:
time: 404 us; the launch traced here: 403 us
  waiting for transfers between devices  194 us (48%)
  blocking collectives  81.4 us (20%)
  starting transfers between devices  39.2 us (10%)
  local copies, waits for them, and re-layouts  36.8 us (9%)
  matrix products  19.5 us (5%)
  between operations  18.2 us (5%)
  other arithmetic  14 us (3%)
    all_to_all x1, waiting for transfers between devices, build_array(): parts_out = lax.all_to_all(val, axis_tag, split_axis=0, concat_axis=0)  87.4 us
    all_gather x1, blocking collectives, side_by_side(): result, at, done = (lax.all_gather(both, axis, axis=dim, tiled=True), 0, [])  52 us
    all_to_all x1, waiting for transfers between devices, per_device(): lax.all_to_all(query_left_factors, POP, split_axis=1, concat_axis=0, tile...  44 us
    all_to_all x1, waiting for transfers between devices, per_device(): lax.all_to_all(o_right, POP, split_axis=2, concat_axis=0, tiled=True)  38.8 us
    all_to_all x2, blocking collectives, build_array(): parts_out = lax.all_to_all(val, axis_tag, split_axis=0, concat_axis=0)  22.9 us
    all_to_all x1, waiting for transfers between devices, summed_on_arrival(): lax.all_to_all(cut_along(shard, dim, devices), axis, 0, 0, tiled=True)  22.5 us
    all_to_all x2, starting transfers between devices, copy_for_each(): return lax.all_to_all(copies, axis, split_axis=0, concat_axis=0, tiled=True)  13.3 us
    unnamed x35, local copies, waits for them, and re-layouts  12 us
  transfers between devices with their start and end apart: 7, of which 5 were waited for; matrix products, arithmetic and copies ran while one was open for 11% of the time, Pallas kernels for 0%

profile of v1, /device:TPU:1, one launch (start us, length us, event | category | flops | bytes accessed | tf_op | source)
XLA Modules:
  0.0 402.6 jit_solution(16368670677369238113)
XLA Ops:
  8.8 11.9 %all_to_all.62 = bf16[4,1,56,896]{3,2,1,0:T(8,128)(2,1)S(1)} all-to-all(bf16[4,1,56,896]{3,2,1,0:T(8,128)(2,1)S(1)} %stack.9), channel_id=1, replica_groups=mesh['pop_0'=4,'pop_1'=8,'pop_2'=2,'mp'=4] {'pop_0'}, dimensions={0} | all-to-all | bytes 802816 | tf_op jit(solution)/shard_map/all_to_all | solution.py:22
  20.7 1.9 stack.10
  22.6 8.3 %all-to-all-start.2 = ((bf16[8,4,56,896]{3,2,1,0:T(8,128)(2,1)}), bf16[8,4,56,896]{3,2,1,0:T(8,128)(2,1)}, u32[]{:S(2)}, u32[]{:S(2)}) async-start(bf16[8,4,56,896]{3,2,1,0:T(8,128)(2,1)} %stack.10), calls=%async_computation.2 | async-start | bytes 6422528 | tf_op jit(solution)/shard_map/all_to_all | solution.py:22
  33.9 87.4 %all-to-all-done.2 = bf16[8,4,56,896]{3,2,1,0:T(8,128)(2,1)} async-done(((bf16[8,4,56,896]{3,2,1,0:T(8,128)(2,1)}), bf16[8,4,56,896]{3,2,1,0:T(8,128)(2,1)}, u32[]{:S(2)}, u32[]{:S(2)}) %all-to-all-start.2) | async-done | bytes 3211296 | tf_op jit(solution)/shard_map/all_to_all | solution.py:22
  121.3 3.5 pad_maximum_fusion
  124.9 11.0 %all_to_all.63 = bf16[2,32,56,896]{3,2,1,0:T(8,128)(2,1)S(1)} all-to-all(bf16[2,32,56,896]{3,2,1,0:T(8,128)(2,1)S(1)} %pad_maximum_fusion), channel_id=1, replica_groups=mesh['pop_0'=4,'pop_1'=8,'pop_2'=2,'mp'=4] {'pop_2'}, dimensions={0} | all-to-all | bytes 12845056 | tf_op jit(solution)/shard_map/all_to_all | solution.py:22
  136.5 2.9 convolution_bitcast_fusion
  139.3 2.2 fusion.3
  148.9 2.6 convolution_convert_fusion
  151.7 5.0 %fusion.29 = f32[256,3584]{1,0:T(8,128)S(1)} fusion(bf16[256,896]{0,1:T(8,128)(2,1)S(1)} %bitcast.109, bf16[896,3584]{0,1:T(8,128)(2,1)} %all-gather.3.cloned.1.call-done), kind=kOutput, calls=%fused_computation.59 | convolution fusion | flops 1644167168 | bytes 10551296 | tf_op jit(solution)/shard_map/mtf,fe->mte/dot_general | solution.py:153
  156.7 3.1 fusion.1
  159.8 3.3 reshape.288
  163.1 1.5 copy.147
  164.6 4.1 %all-to-all-start.4 = ((bf16[4,1,256,896]{3,2,1,0:T(8,128)(2,1)}), bf16[4,1,256,896]{3,2,1,0:T(8,128)(2,1)S(1)}, u32[]{:S(2)}, u32[]{:S(2)}) async-start(bf16[4,1,256,896]{3,2,1,0:T(8,128)(2,1)} %bitcast.101), calls=%async_computation.4 | async-start | bytes 3670016 | tf_op jit(solution)/shard_map/all_to_all | solution.py:53
  169.2 22.5 %all-to-all-done.4 = bf16[4,1,256,896]{3,2,1,0:T(8,128)(2,1)S(1)} async-done(((bf16[4,1,256,896]{3,2,1,0:T(8,128)(2,1)}), bf16[4,1,256,896]{3,2,1,0:T(8,128)(2,1)S(1)}, u32[]{:S(2)}, u32[]{:S(2)}) %all-to-all-start.4) | async-done | bytes 1835040 | tf_op jit(solution)/shard_map/all_to_all | solution.py:53
  193.5 6.5 %all_to_all.64 = f32[4,1,1]{2,1,0:T(1,128)S(1)} all-to-all(f32[4,1,1]{2,1,0:T(1,128)S(1)} %broadcast_in_dim.16), channel_id=1, replica_groups=mesh['pop_0'=4,'pop_1'=8,'pop_2'=2,'mp'=4] {'mp'}, dimensions={0} | all-to-all | bytes 32 | tf_op jit(solution)/shard_map/all_to_all | solution.py:59
  201.9 7.3 %all-to-all-start.6 = ((f32[64,1,1]{2,1,0:T(1,128)}), f32[64,1,1]{2,1,0:T(1,128)S(1)}, u32[]{:S(2)}, u32[]{:S(2)}) async-start(f32[64,1,1]{2,1,0:T(1,128)} %broadcast_in_dim.17), calls=%async_computation.6 | async-start | bytes 65536 | tf_op jit(solution)/shard_map/all_to_all | solution.py:59
  209.2 52.0 %all-gather = bf16[64,1,7168]{2,1,0:T(2,128)(2,1)S(1)} all-gather(bf16[1,1,7168]{2,1,0:T(2,128)(2,1)S(1)} %maximum_bitcast_fusion.2), channel_id=1, replica_groups=mesh['pop_0'=4,'pop_1'=8,'pop_2'=2,'mp'=4] {'pop_0','pop_1','pop_2'}, dimensions={0}, use_global_device_ids=true | all-gather | bytes 931840 | tf_op jit(solution)/shard_map/all_gather | solution.py:73
  261.2 3.2 copy.130
  265.6 7.3 %all-to-all-start.8 = ((bf16[1,4,3584]{1,0,2:T(2,128)(2,1)}), bf16[1,4,3584]{1,0,2:T(2,128)(2,1)S(1)}, u32[]{:S(2)}, u32[]{:S(2)}) async-start(bf16[1,4,3584]{1,0,2:T(2,128)(2,1)} %copy.130), calls=%async_computation.8 | async-start | bytes 3670016 | tf_op jit(solution)/shard_map/all_to_all | solution.py:174
  272.9 2.0 slice_convert_fusion
  275.0 3.2 copy.113
  279.5 38.8 %all-to-all-done.8 = bf16[1,4,3584]{1,0,2:T(2,128)(2,1)S(1)} async-done(((bf16[1,4,3584]{1,0,2:T(2,128)(2,1)}), bf16[1,4,3584]{1,0,2:T(2,128)(2,1)S(1)}, u32[]{:S(2)}, u32[]{:S(2)}) %all-to-all-start.8) | async-done | bytes 28704 | tf_op jit(solution)/shard_map/all_to_all | solution.py:174
  318.3 6.2 %all-to-all-start = ((bf16[1,3584,4]{2,0,1:T(2,128)(2,1)}), bf16[1,3584,4]{2,0,1:T(2,128)(2,1)}, u32[]{:S(2)}, u32[]{:S(2)}) async-start(bf16[1,3584,4]{2,0,1:T(2,128)(2,1)} %copy.113), calls=%async_computation | async-start | bytes 3670016 | tf_op jit(solution)/shard_map/all_to_all | solution.py:173
  325.8 44.0 %all-to-all-done = bf16[1,3584,4]{2,0,1:T(2,128)(2,1)} async-done(((bf16[1,3584,4]{2,0,1:T(2,128)(2,1)}), bf16[1,3584,4]{2,0,1:T(2,128)(2,1)}, u32[]{:S(2)}, u32[]{:S(2)}) %all-to-all-start) | async-done | bytes 28704 | tf_op jit(solution)/shard_map/all_to_all | solution.py:173
  370.4 6.0 %all-to-all-start.7 = ((f32[64,1,1]{2,1,0:T(1,128)}), f32[64,1,1]{2,1,0:T(1,128)S(1)}, u32[]{:S(2)}, u32[]{:S(2)}) async-start(f32[64,1,1]{2,1,0:T(1,128)} %broadcast_in_dim.32), calls=%async_computation.7 | async-start | bytes 65536 | tf_op jit(solution)/shard_map/all_to_all | solution.py:59
  376.4 1.8 copy.128
  379.5 1.8 copy.131
  381.6 3.7 copy.114
  386.2 1.6 multiply_bitcast_fusion
  387.8 2.9 copy.129
  390.7 1.5 reshape.293
  (70 shorter events, 23.5 us)
Async XLA Ops:
  7.2 24.5 %copy-start = (bf16[256,3584]{1,0:T(8,128)(2,1)S(1)}, bf16[256,3584]{1,0:T(8,128)(2,1)}, u32[]{:S(2)}) copy-start(bf16[256,3584]{1,0:T(8,128)(2,1)} %param.11) | copy-start | bytes 5505028
  7.2 144.5 %all-gather.3.cloned.1.call-start = ((), (), s32[]{:S(2)}) async-start(), calls=%async_computation.9 | async-start | bytes 6522880 | tf_op jit(solution)/shard_map/all_gather | solution.py:156
  22.6 9.0 %copy-start.4 = (bf16[3584,128]{1,0:T(8,128)(2,1)S(1)}, bf16[3584,128]{1,0:T(8,128)(2,1)}, u32[]{:S(2)}) copy-start(bf16[3584,128]{1,0:T(8,128)(2,1)} %param.14) | copy-start | bytes 2752516
  22.6 98.7 %all-to-all-start.2 = ((bf16[8,4,56,896]{3,2,1,0:T(8,128)(2,1)}), bf16[8,4,56,896]{3,2,1,0:T(8,128)(2,1)}, u32[]{:S(2)}, u32[]{:S(2)}) async-start(bf16[8,4,56,896]{3,2,1,0:T(8,128)(2,1)} %stack.10), calls=%async_computation.2 | async-start | bytes 6422528 | tf_op jit(solution)/shard_map/all_to_all | solution.py:22
  136.4 2.9 copy-start.9
  136.4 2.9 copy-start.11
  145.0 1.4 copy-start.6
  145.0 1.4 copy-start.7
  147.1 1.3 copy-start.2
  147.1 1.8 copy-start.13
  148.9 2.6 copy-start.12
  151.7 5.0 %copy-start.8 = (bf16[1,4,3584]{2,1,0:T(4,128)(2,1)S(1)}, bf16[1,4,3584]{2,1,0:T(4,128)(2,1)}, u32[]{:S(2)}) copy-start(bf16[1,4,3584]{2,1,0:T(4,128)(2,1)} %param.20) | copy-start | bytes 86020
  164.6 27.1 %all-to-all-start.4 = ((bf16[4,1,256,896]{3,2,1,0:T(8,128)(2,1)}), bf16[4,1,256,896]{3,2,1,0:T(8,128)(2,1)S(1)}, u32[]{:S(2)}, u32[]{:S(2)}) async-start(bf16[4,1,256,896]{3,2,1,0:T(8,128)(2,1)} %bitcast.101), calls=%async_computation.4 | async-start | bytes 3670016 | tf_op jit(solution)/shard_map/all_to_all | solution.py:53
  168.7 23.3 %copy-start.5 = (bf16[256,896]{1,0:T(8,128)(2,1)S(1)}, bf16[256,896]{1,0:T(8,128)(2,1)}, u32[]{:S(2)}) copy-start(bf16[256,896]{1,0:T(8,128)(2,1)} %param.12) | copy-start | bytes 1376260
  201.9 63.7 %all-to-all-start.6 = ((f32[64,1,1]{2,1,0:T(1,128)}), f32[64,1,1]{2,1,0:T(1,128)S(1)}, u32[]{:S(2)}, u32[]{:S(2)}) async-start(f32[64,1,1]{2,1,0:T(1,128)} %broadcast_in_dim.17), calls=%async_computation.6 | async-start | bytes 65536 | tf_op jit(solution)/shard_map/all_to_all | solution.py:59
  265.6 52.7 %all-to-all-start.8 = ((bf16[1,4,3584]{1,0,2:T(2,128)(2,1)}), bf16[1,4,3584]{1,0,2:T(2,128)(2,1)S(1)}, u32[]{:S(2)}, u32[]{:S(2)}) async-start(bf16[1,4,3584]{1,0,2:T(2,128)(2,1)} %copy.130), calls=%async_computation.8 | async-start | bytes 3670016 | tf_op jit(solution)/shard_map/all_to_all | solution.py:174
  272.9 2.0 copy-start.10
  318.3 51.5 %all-to-all-start = ((bf16[1,3584,4]{2,0,1:T(2,128)(2,1)}), bf16[1,3584,4]{2,0,1:T(2,128)(2,1)}, u32[]{:S(2)}, u32[]{:S(2)}) async-start(bf16[1,3584,4]{2,0,1:T(2,128)(2,1)} %copy.113), calls=%async_computation | async-start | bytes 3670016 | tf_op jit(solution)/shard_map/all_to_all | solution.py:173
  370.4 15.3 %all-to-all-start.7 = ((f32[64,1,1]{2,1,0:T(1,128)}), f32[64,1,1]{2,1,0:T(1,128)S(1)}, u32[]{:S(2)}, u32[]{:S(2)}) async-start(f32[64,1,1]{2,1,0:T(1,128)} %broadcast_in_dim.32), calls=%async_computation.7 | async-start | bytes 65536 | tf_op jit(solution)/shard_map/all_to_all | solution.py:59
  381.4 4.9 %copy-start.3 = (f32[64,3584]{0,1:T(8,128)S(1)}, f32[64,3584]{0,1:T(8,128)}, u32[]{:S(2)}) copy-start(f32[64,3584]{0,1:T(8,128)} %copy.128) | copy-start | bytes 2752516
  387.8 6.8 %copy-start.1 = (bf16[256,3584]{1,0:T(8,128)(2,1)S(1)}, bf16[256,3584]{1,0:T(8,128)(2,1)}, u32[]{:S(2)}) copy-start(bf16[256,3584]{1,0:T(8,128)(2,1)} %param.11) | copy-start | bytes 5505028
Sparse Core Ops, SparseCore 0:
  10.7 111.3 all-gather.2
